TPU v7x, 32 devices: a whole 2x2x4 slice. The times are simulated.
32 devices in a mesh: row: 4 (over z), col: 8 (over y, x, core).
Axes of the slice: x: 2, y: 2, z: 4, core: 2. Of those that a mesh axis runs over, the one named last changes fastest.
Arguments:
- operator: bfloat16 [32768, 32768], P('row', 'col'), may hold values from -6 to 6
- right_test: bfloat16 [32768, 256], P('col'), may hold values from -0.03125 to 0.03125
- left_test: bfloat16 [32768, 384], P('row'), may hold values from -0.03125 to 0.03125
Outputs:
- left_factor: bfloat16 [32768, 256], P(('row', 'col'))
- right_factor: bfloat16 [32768, 256], P('col')
All inputs are finite; a program needn't handle non-finite values.
Results may differ from a plain program's by a relative error of at most 0.0015.
Values may be sent and summed in bfloat16 or wider, within the bound.
A program may use at most 192 MiB of HBM per device.

v0:
```python
import jax
import jax.numpy as jnp
from jax import lax
from jax.sharding import PartitionSpec as P


def body(operator, right_test, left_test):
    width_right = right_test.shape[1]
    block_left = jnp.dot(operator, right_test, preferred_element_type=jnp.float32)
    block_core = lax.dot_general(
        left_test.astype(jnp.float32),
        block_left,
        (((0,), (0,)), ((), ())),
        precision=lax.Precision.HIGHEST,
    )
    core_matrix = lax.psum(block_core, ("row", "col"))
    left_share = lax.psum_scatter(block_left, "col", scatter_dimension=0, tiled=True)
    right_whole = lax.psum(
        lax.dot_general(
            operator, left_test, (((0,), (0,)), ((), ())), preferred_element_type=jnp.float32
        ),
        "row",
    )
    gram_plain = jnp.dot(core_matrix.T, core_matrix, precision=lax.Precision.HIGHEST)
    shift_size = 0.001 * jnp.trace(gram_plain) / width_right
    gram_matrix = gram_plain + shift_size * jnp.eye(width_right, dtype=jnp.float32)
    lower_factor = jnp.linalg.cholesky(gram_matrix)
    solve_map = jax.scipy.linalg.cho_solve((lower_factor, True), core_matrix.T)
    right_factor = jnp.dot(right_whole, solve_map.T, precision=lax.Precision.HIGHEST).astype(
        jnp.bfloat16
    )
    return (left_share.astype(jnp.bfloat16), right_factor)


def solution(mesh):
    placed = (P("row", "col"), P("col", None), P("row", None))
    return jax.shard_map(
        body,
        mesh=mesh,
        in_specs=placed,
        out_specs=(P(("row", "col"), None), P("col", None)),
        check_vma=False,
    )
```

profile of v0, /device:TPU:0, one launch (start us, length us, event | category | flops | bytes accessed | tf_op | source)
XLA Modules:
  0.0 432.1 jit_solution(15498314063320386907)
XLA Ops:
  8.0 0.0 copy-start
  8.0 0.0 all-reduce.6.cloned.1.call-start
  8.1 1.5 copy-done
  9.6 28.9 %fusion.17 = f32[8192,256]{1,0:T(8,128)} fusion(bf16[8192,4096]{1,0:T(8,128)(2,1)} %param.3, bf16[4096,256]{1,0:T(8,128)(2,1)S(1)} %copy-done), kind=kOutput, calls=%fused_computation.42 | convolution fusion | flops 17179869184 | bytes 77594624 | tf_op jit(solution)/shard_map/dot_general | solution.py:9
  38.5 10.9 %convolution_bitcast_fusion = f32[384,256]{0,1:T(8,128)} fusion(f32[8192,256]{1,0:T(8,128)} %fusion.17, bf16[8192,384]{1,0:T(8,128)(2,1)} %param.5), kind=kOutput, calls=%fused_computation.3 | convolution fusion | flops 9663676416 | bytes 15073280 | tf_op jit(solution)/shard_map/dot_general | solution.py:10
  49.3 0.0 all-reduce.6.cloned.1.call-update
  49.3 0.0 all-reduce.4.cloned.1.call-start
  49.4 42.3 %fusion.18 = f32[4096,384]{1,0:T(8,128)} fusion(bf16[8192,4096]{1,0:T(8,128)(2,1)} %param.3, bf16[8192,384]{1,0:T(8,128)(2,1)} %param.5), kind=kOutput, calls=%fused_computation.43 | convolution fusion | flops 25769803776 | bytes 79691776 | tf_op jit(solution)/shard_map/dot_general | solution.py:19
  91.7 0.0 all-reduce.4.cloned.1.call-update
  91.7 0.2 reduce-scatter.2.cloned.1.call-start
  91.9 0.3 reduce-scatter.2.cloned.1.call-update
  92.3 96.1 %all-reduce.6.cloned.1.call-done = f32[384,256]{0,1:T(8,128)} async-done(((f32[384,256]{0,1:T(8,128)}), f32[384,256]{0,1:T(8,128)}) %all-reduce.6.cloned.1.call-update) | async-done | bytes 393232 | tf_op jit(solution)/shard_map/psum | solution.py:16
  188.5 2.3 select_reduce_fusion
  190.8 0.1 copy.5
  191.6 0.1 fusion.4
  191.7 11.7 %cholesky.49 = f32[128,128]{1,0:T(8,128)S(1)} custom-call(f32[128,128]{1,0:T(8,128)S(1)} %cholesky.115), custom_call_target="Cholesky" | custom-call | tf_op jit(solution)/shard_map/jit(cholesky)/cholesky | solution.py:27
  203.4 9.8 %custom-call.18 = f32[1,128,128]{1,2,0:T(8,128)S(1)} custom-call(f32[1,128,128]{2,1,0:T(8,128)S(1)} %get-tuple-element.23), custom_call_target="InvertDiagBlocksLowerTriangular" | custom-call | tf_op jit(solution)/shard_map/jit(cholesky)/cholesky | solution.py:27
  213.2 0.2 constant_dynamic-update-slice_fusion.1
  213.5 0.3 convolution_subtract_fusion.2
  213.7 11.7 %cholesky.103 = f32[128,128]{1,0:T(8,128)S(1)} custom-call(f32[128,128]{1,0:T(8,128)S(1)} %convolution_subtract_fusion.2), custom_call_target="Cholesky" | custom-call | tf_op jit(solution)/shard_map/jit(cholesky)/cholesky | solution.py:27
  225.5 0.6 compare_reduce_fusion
  227.4 0.1 triangular_solve.74
  227.4 4.0 while.1
  227.6 0.6 fusion.36
  228.2 1.3 bitcast_dynamic-update-slice_fusion.2
  229.5 0.6 fusion.36
  230.1 1.3 bitcast_dynamic-update-slice_fusion.2
  231.4 19.7 %custom-call.19 = f32[2,128,128]{1,2,0:T(8,128)S(1)} custom-call(f32[2,128,128]{2,1,0:T(8,128)S(1)} %get-tuple-element.9), custom_call_target="InvertDiagBlocksLowerTriangular" | custom-call | tf_op jit(solution)/shard_map/jit(_cho_solve)/triangular_solve | solution.py:28
  251.1 1.3 fusion.5
  252.4 1.2 convolution_subtract_fusion.1
  253.7 0.4 fusion.12
  254.0 0.3 fusion.11
  254.4 0.4 convolution_subtract_fusion
  254.7 0.3 fusion.10
  255.1 157.7 %all-reduce.4.cloned.1.call-done = f32[4096,384]{1,0:T(8,128)} async-done(((f32[4096,384]{1,0:T(8,128)}), f32[4096,384]{1,0:T(8,128)}) %all-reduce.4.cloned.1.call-update) | async-done | bytes 6291472 | tf_op jit(solution)/shard_map/psum | solution.py:18
  412.8 9.8 %convolution_convert_fusion = bf16[4096,256]{1,0:T(8,128)(2,1)} fusion(f32[4096,384]{1,0:T(8,128)} %all-reduce.4.cloned.1.call-done, f32[128,384]{1,0:T(8,128)S(1)} %fusion.11, f32[128,384]{1,0:T(8,128)S(1)} %fusion.10), kind=kOutput, calls=%fused_computation.2 | convolution fusion | flops 4832985088 | bytes 8781824 | tf_op jit(solution)/shard_map/dot_general | solution.py:29
  422.6 0.0 reduce-scatter.2.cloned.1.call-done
  422.6 2.1 convert_element_type.8
  (9 shorter events, 0.1 us)
Async XLA Ops:
  8.0 1.6 copy-start
  8.0 180.4 %all-reduce.6.cloned.1.call-start = ((), (), s32[]{:S(2)}) async-start(), calls=%async_computation.3 | async-start | bytes 786432 | tf_op jit(solution)/shard_map/psum | solution.py:16
  49.3 363.5 %all-reduce.4.cloned.1.call-start = ((), (), s32[]{:S(2)}) async-start(), calls=%async_computation.2 | async-start | bytes 12582912 | tf_op jit(solution)/shard_map/psum | solution.py:18
  91.7 330.9 %reduce-scatter.2.cloned.1.call-start = ((), (), s32[]{:S(2)}) async-start(), calls=%async_computation.1 | async-start | bytes 9437184 | tf_op jit(solution)/shard_map/reduce_scatter | solution.py:17
Sparse Core Ops, SparseCore 0:
  49.5 138.9 all-reduce.5
  190.8 221.9 all-reduce.3
Sparse Core Ops, SparseCore 1:
  95.7 74.4 reduce-scatter.1
where the time goes:
time: 432 us
  waiting for transfers between devices  254 us (59%)
  matrix products  98.5 us (23%)
  other arithmetic  55.8 us (13%)
  between operations  17.5 us (4%)
  local copies, waits for them, and re-layouts  5.54 us (1%)
    psum x1, waiting for transfers between devices, body(): lax.psum(lax.dot_general(operator, left_test, (((0,), (0,)), ((), ())), p...  158 us
    psum x1, waiting for transfers between devices, body(): core_matrix = lax.psum(block_core, ('row', 'col'))  96.1 us
    dot_general x1, matrix products, body(): lax.dot_general(operator, left_test, (((0,), (0,)), ((), ())), preferred_...  42.3 us
    another operation x6, other arithmetic, body(): lower_factor = jnp.linalg.cholesky(gram_matrix)  34 us
    dot_general x1, matrix products, body(): jnp.dot(operator, right_test, preferred_element_type=jnp.float32)  28.9 us
    another operation x3, other arithmetic, body(): solve_map = jax.scipy.linalg.cho_solve((lower_factor, True), core_matrix.T)  19.7 us
    dot_general x1, matrix products, body(): lax.dot_general(left_test.astype(jnp.float32), block_left, (((0,), (0,)),...  10.9 us
    dot_general x1, matrix products, body(): jnp.dot(right_whole, solve_map.T, precision=lax.Precision.HIGHEST)  9.8 us
  transfers between devices with their start and end apart: 3, of which 2 were waited for; matrix products, arithmetic and copies ran while one was open for 27% of the time, Pallas kernels for 0%

commit v1 on v0

--- a/solution.py
+++ b/solution.py
@@ -2,6 +2,12 @@
 import jax.numpy as jnp
 from jax import lax
 from jax.sharding import PartitionSpec as P
+
+
+def add_all(x, axis):
+    parts = lax.all_gather(x, axis, axis=0, tiled=False)
+    result = parts.sum(axis=0)
+    return result
 
 
 def body(operator, right_test, left_test):
@@ -15,7 +21,7 @@
     )
     core_matrix = lax.psum(block_core, ("row", "col"))
     left_share = lax.psum_scatter(block_left, "col", scatter_dimension=0, tiled=True)
-    right_whole = lax.psum(
+    right_whole = add_all(
         lax.dot_general(
             operator, left_test, (((0,), (0,)), ((), ())), preferred_element_type=jnp.float32
         ),

time: 432 us -> 644 us (1.49)
  waiting for transfers between devices: 254 us -> 452 us
  other arithmetic: 55.8 us -> 68.6 us
    all_gather x0 -> x1, waiting for transfers between devices: none -> 357 us  [add_all(): parts = lax.all_gather(x, axis, axis=0, tiled=False)]
    psum x1 -> x0, waiting for transfers between devices: 158 us -> none  [body(): lax.psum(lax.dot_general(operator, left_test, (((0,), (0,)), ((), ())), p...]
    reduce_sum x0 -> x1, other arithmetic: none -> 12.5 us  [add_all(): result = parts.sum(axis=0)]
  transfers between devices with their start and end apart: 3 -> 3, of which waited for: 2 -> 2; matrix products, arithmetic and copies ran while one was open for 27% -> 17% of each run, Pallas kernels for 0% -> 0%
where the time goes in v1:
time: 644 us
  waiting for transfers between devices  452 us (70%)
  matrix products  99.2 us (15%)
  other arithmetic  68.6 us (11%)
  between operations  17.6 us (3%)
    all_gather x1, waiting for transfers between devices, add_all(): parts = lax.all_gather(x, axis, axis=0, tiled=False)  357 us
    psum x1, waiting for transfers between devices, body(): core_matrix = lax.psum(block_core, ('row', 'col'))  95.3 us
    dot_general x1, matrix products, body(): lax.dot_general(operator, left_test, (((0,), (0,)), ((), ())), preferred_...  42.9 us
    another operation x6, other arithmetic, body(): lower_factor = jnp.linalg.cholesky(gram_matrix)  34 us
    dot_general x1, matrix products, body(): jnp.dot(operator, right_test, preferred_element_type=jnp.float32)  28.9 us
    another operation x3, other arithmetic, body(): solve_map = jax.scipy.linalg.cho_solve((lower_factor, True), core_matrix.T)  19.9 us
  transfers between devices with their start and end apart: 3, of which 2 were waited for; matrix products, arithmetic and copies ran while one was open for 17% of the time, Pallas kernels for 0%

profile of v1, /device:TPU:0, one launch (start us, length us, event | category | flops | bytes accessed | tf_op | source)
XLA Modules:
  0.0 643.8 jit_solution(4092182609931731406)
XLA Ops:
  8.0 0.0 copy-start
  8.0 0.0 all-reduce.3.cloned.1.call-start
  8.1 1.5 copy-done
  9.6 28.9 %fusion.17 = f32[8192,256]{1,0:T(8,128)} fusion(bf16[8192,4096]{1,0:T(8,128)(2,1)} %param.3, bf16[4096,256]{1,0:T(8,128)(2,1)S(1)} %copy-done), kind=kOutput, calls=%fused_computation.42 | convolution fusion | flops 17179869184 | bytes 77594624 | tf_op jit(solution)/shard_map/dot_general | solution.py:15
  38.4 10.9 %convolution_bitcast_fusion = f32[384,256]{0,1:T(8,128)} fusion(f32[8192,256]{1,0:T(8,128)} %fusion.17, bf16[8192,384]{1,0:T(8,128)(2,1)} %param.5), kind=kOutput, calls=%fused_computation.3 | convolution fusion | flops 9663676416 | bytes 15073280 | tf_op jit(solution)/shard_map/dot_general | solution.py:16
  49.3 0.0 all-reduce.3.cloned.1.call-update
  49.3 0.0 reduce-scatter.2.cloned.1.call-start
  49.4 0.5 reduce-scatter.2.cloned.1.call-update
  49.9 0.0 all-gather.3.cloned.1.call-start
  50.0 42.9 %fusion.18 = f32[4096,384]{1,0:T(8,128)} fusion(bf16[8192,4096]{1,0:T(8,128)(2,1)} %param.3, bf16[8192,384]{1,0:T(8,128)(2,1)} %param.5), kind=kOutput, calls=%fused_computation.43 | convolution fusion | flops 25769803776 | bytes 79691776 | tf_op jit(solution)/shard_map/dot_general | solution.py:25
  92.9 0.0 all-gather.3.cloned.1.call-update
  92.9 95.3 %all-reduce.3.cloned.1.call-done = f32[384,256]{0,1:T(8,128)} async-done(((f32[384,256]{0,1:T(8,128)}), f32[384,256]{0,1:T(8,128)}) %all-reduce.3.cloned.1.call-update) | async-done | bytes 393232 | tf_op jit(solution)/shard_map/psum | solution.py:22
  188.2 2.3 select_reduce_fusion
  190.5 0.1 copy.5
  191.3 0.1 fusion.4
  191.4 11.7 %cholesky.49 = f32[128,128]{1,0:T(8,128)S(1)} custom-call(f32[128,128]{1,0:T(8,128)S(1)} %cholesky.115), custom_call_target="Cholesky" | custom-call | tf_op jit(solution)/shard_map/jit(cholesky)/cholesky | solution.py:33
  203.2 9.8 %custom-call.18 = f32[1,128,128]{1,2,0:T(8,128)S(1)} custom-call(f32[1,128,128]{2,1,0:T(8,128)S(1)} %get-tuple-element.23), custom_call_target="InvertDiagBlocksLowerTriangular" | custom-call | tf_op jit(solution)/shard_map/jit(cholesky)/cholesky | solution.py:33
  213.0 0.2 constant_dynamic-update-slice_fusion.1
  213.2 0.3 convolution_subtract_fusion.2
  213.5 11.7 %cholesky.103 = f32[128,128]{1,0:T(8,128)S(1)} custom-call(f32[128,128]{1,0:T(8,128)S(1)} %convolution_subtract_fusion.2), custom_call_target="Cholesky" | custom-call | tf_op jit(solution)/shard_map/jit(cholesky)/cholesky | solution.py:33
  225.2 0.7 compare_reduce_fusion
  227.3 0.1 triangular_solve.74
  227.4 4.1 while.1
  227.4 0.6 fusion.36
  228.0 1.4 bitcast_dynamic-update-slice_fusion.2
  229.5 0.6 fusion.36
  230.1 1.4 bitcast_dynamic-update-slice_fusion.2
  231.5 19.9 %custom-call.19 = f32[2,128,128]{1,2,0:T(8,128)S(1)} custom-call(f32[2,128,128]{2,1,0:T(8,128)S(1)} %get-tuple-element.9), custom_call_target="InvertDiagBlocksLowerTriangular" | custom-call | tf_op jit(solution)/shard_map/jit(_cho_solve)/triangular_solve | solution.py:34
  251.4 1.3 fusion.5
  252.7 1.2 convolution_subtract_fusion.1
  253.9 0.4 fusion.12
  254.3 0.3 fusion.11
  254.6 0.4 convolution_subtract_fusion
  255.0 0.3 fusion.10
  255.3 0.0 reduce-scatter.2.cloned.1.call-done
  255.4 2.1 convert_element_type.8
  257.4 356.6 %all-gather.3.cloned.1.call-done = f32[16384,384]{1,0:T(8,128)} async-done(((f32[4096,384]{1,0:T(8,128)}), f32[16384,384]{1,0:T(8,128)}) %all-gather.3.cloned.1.call-update) | async-done | bytes 25165840 | tf_op jit(solution)/shard_map/all_gather | solution.py:8
  614.1 12.5 %reduce_sum.19 = f32[4096,384]{1,0:T(8,128)} reduce(f32[4,4096,384]{2,1,0:T(8,128)} %bitcast.51, f32[]{:T(128)} %constant.93.clone.1), dimensions={0}, to_apply=%region_1.0 | reduce | flops 4718592 | bytes 31457284 | tf_op jit(solution)/shard_map/reduce_sum | solution.py:9
  626.5 9.8 %convolution_convert_fusion = bf16[4096,256]{1,0:T(8,128)(2,1)} fusion(f32[4096,384]{1,0:T(8,128)} %reduce_sum.19, f32[128,384]{1,0:T(8,128)S(1)} %fusion.11, f32[128,384]{1,0:T(8,128)S(1)} %fusion.10), kind=kOutput, calls=%fused_computation.2 | convolution fusion | flops 4832985088 | bytes 8781824 | tf_op jit(solution)/shard_map/dot_general | solution.py:35
  (9 shorter events, 0.1 us)
Async XLA Ops:
  8.0 1.6 copy-start
  8.0 180.2 %all-reduce.3.cloned.1.call-start = ((), (), s32[]{:S(2)}) async-start(), calls=%async_computation.2 | async-start | bytes 786432 | tf_op jit(solution)/shard_map/psum | solution.py:22
  49.3 206.0 %reduce-scatter.2.cloned.1.call-start = ((), (), s32[]{:S(2)}) async-start(), calls=%async_computation.1 | async-start | bytes 9437184 | tf_op jit(solution)/shard_map/reduce_scatter | solution.py:23
  49.9 564.2 %all-gather.3.cloned.1.call-start = ((), (), s32[]{:S(2)}) async-start(), calls=%async_computation.3 | async-start | bytes 31457280 | tf_op jit(solution)/shard_map/all_gather | solution.py:8
Sparse Core Ops, SparseCore 0:
  49.4 138.7 all-reduce.2
  189.8 424.2 all-gather.2
Sparse Core Ops, SparseCore 1:
  53.3 74.4 reduce-scatter.1

commit v2 on v0

--- a/solution.py
+++ b/solution.py
@@ -13,7 +13,8 @@
         (((0,), (0,)), ((), ())),
         precision=lax.Precision.HIGHEST,
     )
-    core_matrix = lax.psum(block_core, ("row", "col"))
+    half = lax.psum(block_core, "row")
+    core_matrix = lax.psum(half, "col")
     left_share = lax.psum_scatter(block_left, "col", scatter_dimension=0, tiled=True)
     right_whole = lax.psum(
         lax.dot_general(

time: 432 us -> 468 us (1.083)
  waiting for transfers between devices: 254 us -> 295 us
    psum x1, waiting for transfers between devices: 158 us -> 238 us  [body(): lax.psum(lax.dot_general(operator, left_test, (((0,), (0,)), ((), ())), p...]
    psum x1, waiting for transfers between devices: 96.1 us -> 55.6 us  [body(): core_matrix = lax.psum(half, 'col')]
  transfers between devices with their start and end apart: 3 -> 3, of which waited for: 2 -> 2; matrix products, arithmetic and copies ran while one was open for 27% -> 16% of each run, Pallas kernels for 0% -> 0%
where the time goes in v2:
time: 468 us
  waiting for transfers between devices  295 us (63%)
  matrix products  95.4 us (20%)
  other arithmetic  55.8 us (12%)
  between operations  15.8 us (3%)
  local copies, waits for them, and re-layouts  5.69 us (1%)
    psum x1, waiting for transfers between devices, body(): lax.psum(lax.dot_general(operator, left_test, (((0,), (0,)), ((), ())), p...  238 us
    psum x1, waiting for transfers between devices, body(): core_matrix = lax.psum(half, 'col')  55.6 us
    dot_general x1, matrix products, body(): lax.dot_general(operator, left_test, (((0,), (0,)), ((), ())), preferred_...  42.4 us
    another operation x6, other arithmetic, body(): lower_factor = jnp.linalg.cholesky(gram_matrix)  34 us
    dot_general x1, matrix products, body(): jnp.dot(operator, right_test, preferred_element_type=jnp.float32)  28.9 us
    another operation x3, other arithmetic, body(): solve_map = jax.scipy.linalg.cho_solve((lower_factor, True), core_matrix.T)  19.7 us
    dot_general x1, matrix products, body(): jnp.dot(right_whole, solve_map.T, precision=lax.Precision.HIGHEST)  9.81 us
  transfers between devices with their start and end apart: 3, of which 2 were waited for; matrix products, arithmetic and copies ran while one was open for 16% of the time, Pallas kernels for 0%

profile of v2, /device:TPU:0, one launch (start us, length us, event | category | flops | bytes accessed | tf_op | source)
XLA Modules:
  0.0 467.8 jit_solution(5867249001530297164)
XLA Ops:
  7.2 0.0 copy-start
  7.2 0.0 all-reduce.7.cloned.1.call-start
  7.2 1.5 copy-done
  8.8 28.9 %fusion.17 = f32[8192,256]{1,0:T(8,128)} fusion(bf16[8192,4096]{1,0:T(8,128)(2,1)} %param.3, bf16[4096,256]{1,0:T(8,128)(2,1)S(1)} %copy-done), kind=kOutput, calls=%fused_computation.42 | convolution fusion | flops 17179869184 | bytes 77594624 | tf_op jit(solution)/shard_map/dot_general | solution.py:9
  37.6 0.0 copy-start.1
  37.6 0.0 copy-start.2
  37.6 42.4 %fusion.18 = f32[4096,384]{1,0:T(8,128)} fusion(bf16[8192,4096]{1,0:T(8,128)(2,1)} %param.3, bf16[8192,384]{1,0:T(8,128)(2,1)} %param.5), kind=kOutput, calls=%fused_computation.43 | convolution fusion | flops 25769803776 | bytes 79691776 | tf_op jit(solution)/shard_map/dot_general | solution.py:20
  80.1 0.0 copy-done.1
  80.1 0.0 copy-done.2
  80.1 7.4 %convolution_bitcast_fusion = f32[384,256]{0,1:T(8,128)} fusion(f32[8192,256]{1,0:T(8,128)S(1)} %copy-done.1, bf16[8192,384]{1,0:T(8,128)(2,1)S(1)} %copy-done.2), kind=kOutput, calls=%fused_computation.3 | convolution fusion | flops 9663676416 | bytes 15073280 | tf_op jit(solution)/shard_map/dot_general | solution.py:10
  87.5 0.0 all-reduce.7.cloned.1.call-update
  87.6 0.0 all-reduce.5.cloned.1.call-start
  87.6 238.4 %all-reduce.7.cloned.1.call-done = (f32[4096,384]{1,0:T(8,128)}, f32[384,256]{0,1:T(8,128)}) async-done(((f32[4096,384]{1,0:T(8,128)}, f32[384,256]{0,1:T(8,128)}), (f32[4096,384]{1,0:T(8,128)}, f32[384,256]{0,1:T(8,128)})) %all-reduce.7.cloned.1.call-update) | async-done | bytes 6684688 | tf_op jit(solution)/shard_map/psum | solution.py:19
  326.0 0.0 all-reduce.5.cloned.1.call-update
  326.1 0.3 reduce-scatter.2.cloned.1.call-start
  326.3 0.5 reduce-scatter.2.cloned.1.call-update
  326.8 55.6 %all-reduce.5.cloned.1.call-done = f32[384,256]{0,1:T(8,128)} async-done(((f32[384,256]{0,1:T(8,128)}), f32[384,256]{0,1:T(8,128)}) %all-reduce.5.cloned.1.call-update) | async-done | bytes 393232 | tf_op jit(solution)/shard_map/psum | solution.py:17
  382.4 2.5 select_reduce_fusion
  384.9 0.1 copy.5
  385.6 0.1 fusion.4
  385.7 11.7 %cholesky.49 = f32[128,128]{1,0:T(8,128)S(1)} custom-call(f32[128,128]{1,0:T(8,128)S(1)} %cholesky.115), custom_call_target="Cholesky" | custom-call | tf_op jit(solution)/shard_map/jit(cholesky)/cholesky | solution.py:28
  397.5 9.8 %custom-call.18 = f32[1,128,128]{1,2,0:T(8,128)S(1)} custom-call(f32[1,128,128]{2,1,0:T(8,128)S(1)} %get-tuple-element.25), custom_call_target="InvertDiagBlocksLowerTriangular" | custom-call | tf_op jit(solution)/shard_map/jit(cholesky)/cholesky | solution.py:28
  407.3 0.2 constant_dynamic-update-slice_fusion.1
  407.5 0.3 convolution_subtract_fusion.2
  407.8 11.7 %cholesky.103 = f32[128,128]{1,0:T(8,128)S(1)} custom-call(f32[128,128]{1,0:T(8,128)S(1)} %convolution_subtract_fusion.2), custom_call_target="Cholesky" | custom-call | tf_op jit(solution)/shard_map/jit(cholesky)/cholesky | solution.py:28
  419.5 0.7 compare_reduce_fusion
  421.5 0.1 triangular_solve.74
  421.6 4.2 while.1
  421.8 0.6 fusion.36
  422.4 1.4 bitcast_dynamic-update-slice_fusion.2
  423.8 0.6 fusion.36
  424.4 1.4 bitcast_dynamic-update-slice_fusion.2
  425.8 19.7 %custom-call.19 = f32[2,128,128]{1,2,0:T(8,128)S(1)} custom-call(f32[2,128,128]{2,1,0:T(8,128)S(1)} %get-tuple-element.9), custom_call_target="InvertDiagBlocksLowerTriangular" | custom-call | tf_op jit(solution)/shard_map/jit(_cho_solve)/triangular_solve | solution.py:29
  445.4 1.3 fusion.5
  446.7 1.2 convolution_subtract_fusion.1
  448.0 0.4 fusion.12
  448.4 0.3 fusion.11
  448.7 0.4 convolution_subtract_fusion
  449.1 0.3 fusion.10
  449.4 9.8 %convolution_convert_fusion = bf16[4096,256]{1,0:T(8,128)(2,1)} fusion(f32[4096,384]{1,0:T(8,128)} %get-tuple-element.18, f32[128,384]{1,0:T(8,128)S(1)} %fusion.11, f32[128,384]{1,0:T(8,128)S(1)} %fusion.10), kind=kOutput, calls=%fused_computation.2 | convolution fusion | flops 4832985088 | bytes 8781824 | tf_op jit(solution)/shard_map/dot_general | solution.py:30
  459.2 0.0 reduce-scatter.2.cloned.1.call-done
  459.2 2.1 convert_element_type.8
  (9 shorter events, 0.1 us)
Async XLA Ops:
  7.2 1.6 copy-start
  7.2 318.9 %all-reduce.7.cloned.1.call-start = ((), (), s32[]{:S(2)}) async-start(), calls=%async_computation.3 | async-start | bytes 13369344 | tf_op jit(solution)/shard_map/psum | solution.py:19
  37.6 42.5 %copy-start.1 = (f32[8192,256]{1,0:T(8,128)S(1)}, f32[8192,256]{1,0:T(8,128)}, u32[]{:S(2)}) copy-start(f32[8192,256]{1,0:T(8,128)} %fusion.17) | copy-start | bytes 25165828
  37.6 42.5 %copy-start.2 = (bf16[8192,384]{1,0:T(8,128)(2,1)S(1)}, bf16[8192,384]{1,0:T(8,128)(2,1)}, u32[]{:S(2)}) copy-start(bf16[8192,384]{1,0:T(8,128)(2,1)} %param.5) | copy-start | bytes 18874372
  87.6 294.8 %all-reduce.5.cloned.1.call-start = ((), (), s32[]{:S(2)}) async-start(), calls=%async_computation.2 | async-start | bytes 786432 | tf_op jit(solution)/shard_map/psum | solution.py:17
  326.1 133.1 %reduce-scatter.2.cloned.1.call-start = ((), (), s32[]{:S(2)}) async-start(), calls=%async_computation.1 | async-start | bytes 9437184 | tf_op jit(solution)/shard_map/reduce_scatter | solution.py:18
Sparse Core Ops, SparseCore 0:
  87.7 238.3 all-reduce.6
  329.1 53.2 all-reduce.4
  385.9 70.9 reduce-scatter.1
